TPU v7x, 32 devices: a whole 2x2x4 slice. The times are simulated.
32 devices in a mesh: outer: 4 (over y, x), inner: 8 (over z, core).
Axes of the slice: x: 2, y: 2, z: 4, core: 2. Of those that a mesh axis runs over, the one named last changes fastest.
Arguments:
- ratings: bfloat16 [32768, 2048], P(('outer', 'inner')), may hold values from -4 to 4
- rating_weights: bfloat16 [32768, 2048], P(('outer', 'inner')), may hold values from 0 to 1.5, as said below
- user_counts: int32 [32768], P(('outer', 'inner')), may hold values from 16 to 96
- item_counts: int32 [8192], replicated, may hold values from 32 to 256
- users: bfloat16 [32768, 256], P(('outer', 'inner')), may hold values from -1.5 to 1.5
- user_moment: float32 [32768, 256], P(('outer', 'inner')), may hold values from -0.3 to 0.3
- items: bfloat16 [8192, 256], P(('outer', 'inner')), may hold values from -1.5 to 1.5
- item_moment: bfloat16 [8192, 256], P(('outer', 'inner')), may hold values from -0.29882812 to 0.29882812
Outputs:
- new_users: bfloat16 [32768, 256], P(('outer', 'inner'))
- new_user_moment: float32 [32768, 256], P(('outer', 'inner'))
- new_items: bfloat16 [8192, 256], P(('outer', 'inner'))
- new_item_moment: bfloat16 [8192, 256], P(('outer', 'inner'))
Inputs may be any that keep to these rules, and one draw needn't show every extreme that they name: `rating_weights`: A weight is 0 exactly where the rating is not observed, else positive.
All inputs are finite; a program needn't handle non-finite values.
Results may differ from a plain program's by a relative error of at most 0.011.
Values may be sent and summed in bfloat16 or wider, within the bound.
A program may use at most 128 MiB of HBM per device.

v0:
```python
import functools

import jax
import jax.numpy as jnp
from jax import lax
from jax.experimental import pallas as pl
from jax.experimental.pallas import tpu as pltpu
from jax.sharding import PartitionSpec as P

STEPS = 8
CHUNKS = 2
TILE = 256
LANES = 128
MESH = pl.DeviceIdType.MESH

learn_rate = 0.3
moment_rate = 0.9
decay_rate = 0.02


def kernel(
    n_outer, n_inner,
    x_hbm, w_hbm, uc_hbm, ic_hbm, u_hbm, p_hbm, v_hbm, q_hbm,
    u_out, p_out, v_out, q_out,
    x, w, uc, ic, u, ut, p, v0, q0, vt, qt, vn, qn, mis, rcu, counts,
    x_sem, w_sem, in_sem, send_sem, recv_sem, out_sem,
):
    outer = lax.axis_index("outer")
    inner = lax.axis_index("inner")
    i_right, i_left = lax.rem(inner + 1, n_inner), lax.rem(inner + n_inner - 1, n_inner)
    o_right, o_left = lax.rem(outer + 1, n_outer), lax.rem(outer + n_outer - 1, n_outer)

    users, rank = u.shape
    block = v0.shape[0]
    part = block // CHUNKS
    tile = min(TILE, users)

    def load(src, dst, sem):
        copy = pltpu.make_async_copy(src, dst, sem)
        copy.start()
        return copy

    v_load = load(v_hbm, v0, in_sem.at[0])
    u_load = load(u_hbm, u, in_sem.at[1])
    loads = []
    for s in range(STEPS):
        cols = slice(s * block, (s + 1) * block)
        loads.append((
            load(x_hbm.at[:, cols], x.at[s], x_sem.at[s]),
            load(w_hbm.at[:, cols], w.at[s], w_sem.at[s]),
        ))
        if s == 0:
            q_load = load(q_hbm, q0, in_sem.at[2])
            ic_load = load(ic_hbm, ic, in_sem.at[3])
            uc_load = load(uc_hbm, uc, in_sem.at[4])
            p_load = load(p_hbm, p, in_sem.at[5])

    barrier = pltpu.get_barrier_semaphore()
    for where in ((outer, i_left), (outer, i_right), (o_left, inner), (o_right, inner)):
        pl.semaphore_signal(barrier, inc=1, device_id=where, device_id_type=MESH)

    v_load.wait()
    vt[0] = v0[...].T
    u_load.wait()
    for t in range(users // tile):
        rows = slice(t * tile, (t + 1) * tile)
        ut[:, rows] = u[rows, :].T
    q_load.wait()
    qt[0] = q0[...].T

    ic_load.wait()
    per = block // LANES
    for s in range(STEPS):
        late = 1 if s >= STEPS // 2 else 0
        o_from = lax.rem(outer - late + n_outer, n_outer)
        i_from = lax.rem(inner - (s - late) + n_inner * STEPS, n_inner)
        first = (o_from * n_inner + i_from) * per
        for j in range(per):
            row = ic[pl.ds(first + j, 1), :].astype(jnp.float32)
            counts[s : s + 1, j * LANES : (j + 1) * LANES] = 1.0 / row
    uc_load.wait()
    flipped = (1.0 / uc[...].astype(jnp.float32)).T
    for j in range(users // LANES):
        rcu[j * LANES : (j + 1) * LANES, :] = jnp.broadcast_to(flipped[:, j : j + 1], (LANES, LANES))

    sends = []
    outs = []
    arrivals = [None]
    for s in range(STEPS):
        last = s == STEPS - 1
        if s == STEPS // 2 - 1:
            target = (o_right, inner)
        else:
            target = (outer, i_right)
        if s == 0:
            loads[0][0].wait()
            loads[0][1].wait()
        else:
            loads[s][0].wait()
            loads[s][1].wait()
        copies = []
        for k in range(CHUNKS):
            cols = slice(k * part, (k + 1) * part)
            if s > 0:
                arrivals[s][k][0].wait_recv()
            items = vt[s, :, cols]
            for t in range(users // tile):
                rows = slice(t * tile, (t + 1) * tile)
                pred = jnp.dot(u[rows, :], items, preferred_element_type=jnp.float32)
                rated = x[s, rows, cols].astype(jnp.float32)
                weight = w[s, rows, cols].astype(jnp.float32)
                mis[rows, cols] = (weight * (pred - rated)).astype(jnp.bfloat16)
            product = jnp.dot(ut[...], mis[:, cols], preferred_element_type=jnp.float32)
            if s > 0:
                arrivals[s][k][1].wait_recv()
            old = items.astype(jnp.float32)
            grad = product * counts[s : s + 1, cols] + decay_rate * old
            moment = (moment_rate * qt[s, :, cols].astype(jnp.float32) + grad).astype(jnp.bfloat16)
            qn[s, :, cols] = moment
            vn[s, :, cols] = (old - learn_rate * moment.astype(jnp.float32)).astype(jnp.bfloat16)
            if not last:
                if s == 0 and k == 0:
                    pl.semaphore_wait(barrier, 4)
                pair = []
                for j, (src, dst) in enumerate(((vn, vt), (qn, qt))):
                    copy = pltpu.make_async_remote_copy(
                        src_ref=src.at[s, :, cols],
                        dst_ref=dst.at[s + 1, :, cols],
                        send_sem=send_sem.at[s, k, j],
                        recv_sem=recv_sem.at[s, k, j],
                        device_id=target,
                        device_id_type=MESH,
                    )
                    copy.start()
                    pair.append(copy)
                copies.append(pair)
            else:
                v0[cols, :] = vn[s, :, cols].T
                q0[cols, :] = qn[s, :, cols].T
                for j, (src, dst) in enumerate(((v0, v_out), (q0, q_out))):
                    outs.append(load(src.at[cols], dst.at[cols], out_sem.at[0, 2 * k + j]))
        arrivals.append(copies)
        sends.append(copies)
        if s == 0:
            p_load.wait()
        for t in range(users // tile):
            rows = slice(t * tile, (t + 1) * tile)
            total = lax.dot_general(
                mis[rows, :], vt[s], (((1,), (1,)), ((), ())), preferred_element_type=jnp.float32
            )
            old = u[rows, :].astype(jnp.float32)
            scale = jnp.concatenate([rcu[rows, :]] * (rank // LANES), axis=1)
            moment = moment_rate * p[rows, :] + (total * scale + decay_rate * old)
            p[rows, :] = moment
            new = (old - learn_rate * moment).astype(jnp.bfloat16)
            u[rows, :] = new
            if last:
                outs.append(load(u.at[rows], u_out.at[rows], out_sem.at[1, t]))
                outs.append(load(p.at[rows], p_out.at[rows], out_sem.at[2, t]))
            else:
                ut[:, rows] = new.T
    for copies in sends:
        for pair in copies:
            for copy in pair:
                copy.wait_send()
    for copy in outs:
        copy.wait()


def body(ratings, rating_weights, user_counts, item_counts, users, user_moment, items, item_moment):
    n_outer = lax.axis_size("outer")
    n_inner = lax.axis_size("inner")
    n_users, rank = users.shape
    block = items.shape[0]
    n_items = item_counts.shape[0]
    tiles = max(n_users // min(TILE, n_users), 2 * CHUNKS)
    bf16, f32, i32 = jnp.bfloat16, jnp.float32, jnp.int32
    return pl.pallas_call(
        functools.partial(kernel, n_outer, n_inner),
        out_shape=(
            jax.ShapeDtypeStruct(users.shape, bf16),
            jax.ShapeDtypeStruct(user_moment.shape, f32),
            jax.ShapeDtypeStruct(items.shape, bf16),
            jax.ShapeDtypeStruct(item_moment.shape, bf16),
        ),
        in_specs=[pl.BlockSpec(memory_space=pltpu.HBM)] * 8,
        out_specs=(pl.BlockSpec(memory_space=pl.ANY),) * 4,
        scratch_shapes=[
            pltpu.VMEM((STEPS, n_users, block), bf16),
            pltpu.VMEM((STEPS, n_users, block), bf16),
            pltpu.VMEM((n_users // LANES, LANES), i32),
            pltpu.VMEM((n_items // LANES, LANES), i32),
            pltpu.VMEM((n_users, rank), bf16),
            pltpu.VMEM((rank, n_users), bf16),
            pltpu.VMEM((n_users, rank), f32),
            pltpu.VMEM((block, rank), bf16),
            pltpu.VMEM((block, rank), bf16),
            pltpu.VMEM((STEPS, rank, block), bf16),
            pltpu.VMEM((STEPS, rank, block), bf16),
            pltpu.VMEM((STEPS, rank, block), bf16),
            pltpu.VMEM((STEPS, rank, block), bf16),
            pltpu.VMEM((n_users, block), bf16),
            pltpu.VMEM((n_users, LANES), f32),
            pltpu.VMEM((STEPS, block), f32),
            pltpu.SemaphoreType.DMA((STEPS,)),
            pltpu.SemaphoreType.DMA((STEPS,)),
            pltpu.SemaphoreType.DMA((6,)),
            pltpu.SemaphoreType.DMA((STEPS, CHUNKS, 2)),
            pltpu.SemaphoreType.DMA((STEPS, CHUNKS, 2)),
            pltpu.SemaphoreType.DMA((3, tiles)),
        ],
        compiler_params=pltpu.CompilerParams(
            collective_id=0, has_side_effects=True, vmem_limit_bytes=48 * 1024 * 1024
        ),
    )(
        ratings,
        rating_weights,
        user_counts.reshape(n_users // LANES, LANES),
        item_counts.reshape(n_items // LANES, LANES),
        users,
        user_moment,
        items,
        item_moment,
    )


def solution(mesh):
    spread = P(("outer", "inner"), None)
    in_specs = (spread, spread, P(("outer", "inner")), P(), spread, spread, spread, spread)
    return jax.shard_map(
        body, mesh=mesh, in_specs=in_specs, out_specs=(spread,) * 4, check_vma=False
    )
```

profile of v0, /device:TPU:0, one launch (start us, length us, event | category | flops | bytes accessed | tf_op | source)
XLA Modules:
  0.0 42.8 jit_solution(9410067712837383733)
XLA Ops:
  0.6 0.0 copy-start
  0.6 1.2 %copy-done = f32[1024,256]{1,0:T(8,128)S(1)} copy-done((f32[1024,256]{1,0:T(8,128)S(1)}, f32[1024,256]{1,0:T(8,128)}, u32[]{:S(2)}) %copy-start) | copy-done | bytes 1048600
  1.9 0.0 copy-start.1
  1.9 1.0 %copy-done.1 = bf16[1024,256]{1,0:T(8,128)(2,1)S(1)} copy-done((bf16[1024,256]{1,0:T(8,128)(2,1)S(1)}, bf16[1024,256]{1,0:T(8,128)(2,1)}, u32[]{:S(2)}) %copy-start.1) | copy-done | bytes 524312
  2.9 0.0 copy-start.2
  2.9 0.9 %copy-done.2 = bf16[256,256]{1,0:T(8,128)(2,1)S(1)} copy-done((bf16[256,256]{1,0:T(8,128)(2,1)S(1)}, bf16[256,256]{1,0:T(8,128)(2,1)}, u32[]{:S(2)}) %copy-start.2) | copy-done | bytes 131096
  3.8 0.0 copy-start.3
  3.8 0.9 %copy-done.3 = bf16[256,256]{1,0:T(8,128)(2,1)S(1)} copy-done((bf16[256,256]{1,0:T(8,128)(2,1)S(1)}, bf16[256,256]{1,0:T(8,128)(2,1)}, u32[]{:S(2)}) %copy-start.3) | copy-done | bytes 131096
  4.7 0.0 copy-start.4
  4.7 0.8 %copy-done.4 = s32[8192]{0:T(1024)S(1)} copy-done((s32[8192]{0:T(1024)S(1)}, s32[8192]{0:T(1024)}, u32[]{:S(2)}) %copy-start.4) | copy-done | bytes 32792
  5.5 0.0 copy-start.5
  5.5 0.7 %copy-done.5 = s32[1024]{0:T(1024)S(1)} copy-done((s32[1024]{0:T(1024)S(1)}, s32[1024]{0:T(1024)}, u32[]{:S(2)}) %copy-start.5) | copy-done | bytes 4120
  6.2 33.5 %shard_map.111 = (bf16[1024,256]{1,0:T(8,128)(2,1)S(1)}, f32[1024,256]{1,0:T(8,128)S(1)}, bf16[256,256]{1,0:T(8,128)(2,1)S(1)}, bf16[256,256]{1,0:T(8,128)(2,1)S(1)}) custom-call(bf16[1024,2048]{1,0:T(8,128)(2,1)} %x_hbm.1, bf16[1024,2048]{1,0:T(8,128)(2,1)} %w_hbm.1, s32[8,128]{1,0:T(8,128)S(1)} %bitcast.3, s32[64,128]{1,0:T(8,128)S(1)} %bitcast.2, ...), custom_call_target="tpu_custom_call" | custom-call | tf_op jit(solution)/shard_map/pallas_call | solution.py:178
  39.7 0.8 %copy.16 = bf16[1024,256]{1,0:T(8,128)(2,1)} copy(bf16[1024,256]{1,0:T(8,128)(2,1)S(1)} %get-tuple-element.8) | data formatting | bytes 1048576
  40.5 1.0 %copy.17 = f32[1024,256]{1,0:T(8,128)} copy(f32[1024,256]{1,0:T(8,128)S(1)} %get-tuple-element.9) | data formatting | bytes 2097152
  41.5 0.7 %copy.18 = bf16[256,256]{1,0:T(8,128)(2,1)} copy(bf16[256,256]{1,0:T(8,128)(2,1)S(1)} %get-tuple-element.10) | data formatting | bytes 262144
  42.1 0.7 %copy.19 = bf16[256,256]{1,0:T(8,128)(2,1)} copy(bf16[256,256]{1,0:T(8,128)(2,1)S(1)} %get-tuple-element.11) | data formatting | bytes 262144
Async XLA Ops:
  0.6 1.2 %copy-start = (f32[1024,256]{1,0:T(8,128)S(1)}, f32[1024,256]{1,0:T(8,128)}, u32[]{:S(2)}) copy-start(f32[1024,256]{1,0:T(8,128)} %p_hbm.1) | copy-start | bytes 3145732
  1.9 1.0 %copy-start.1 = (bf16[1024,256]{1,0:T(8,128)(2,1)S(1)}, bf16[1024,256]{1,0:T(8,128)(2,1)}, u32[]{:S(2)}) copy-start(bf16[1024,256]{1,0:T(8,128)(2,1)} %u_hbm.1) | copy-start | bytes 1572868
  2.9 0.9 %copy-start.2 = (bf16[256,256]{1,0:T(8,128)(2,1)S(1)}, bf16[256,256]{1,0:T(8,128)(2,1)}, u32[]{:S(2)}) copy-start(bf16[256,256]{1,0:T(8,128)(2,1)} %v_hbm.1) | copy-start | bytes 393220
  3.8 0.9 %copy-start.3 = (bf16[256,256]{1,0:T(8,128)(2,1)S(1)}, bf16[256,256]{1,0:T(8,128)(2,1)}, u32[]{:S(2)}) copy-start(bf16[256,256]{1,0:T(8,128)(2,1)} %q_hbm.1) | copy-start | bytes 393220
  4.7 0.8 %copy-start.4 = (s32[8192]{0:T(1024)S(1)}, s32[8192]{0:T(1024)}, u32[]{:S(2)}) copy-start(s32[8192]{0:T(1024)} %param.11) | copy-start | bytes 98308
  5.5 0.7 %copy-start.5 = (s32[1024]{0:T(1024)S(1)}, s32[1024]{0:T(1024)}, u32[]{:S(2)}) copy-start(s32[1024]{0:T(1024)} %param.10) | copy-start | bytes 12292
where the time goes:
time: 43.1 us; the launch traced here: 42.8 us
  Pallas kernels  33.5 us (78%)
  local copies, waits for them, and re-layouts  8.58 us (20%)
  between operations  0.66 us (2%)
    pallas_call x1, Pallas kernels, body(): pl.pallas_call(functools.partial(kernel, n_outer, n_inner), out_shape=(ja...  33.5 us
    unnamed x16, local copies, waits for them, and re-layouts  8.58 us

commit v1 on v0

v1 whole, which is shorter than its diff:
```python
import functools

import jax
import jax.numpy as jnp
from jax import lax
from jax.experimental import pallas as pl
from jax.experimental.pallas import tpu as pltpu
from jax.sharding import PartitionSpec as P

STEPS = 8
HALF = STEPS // 2
CHUNKS = 2
TILE = 256
LANES = 128
MESH = pl.DeviceIdType.MESH
BF16, F32 = jnp.bfloat16, jnp.float32

learn_rate = 0.3
moment_rate = 0.9
decay_rate = 0.02


def load(src, dst, sem):
    copy = pltpu.make_async_copy(src, dst, sem)
    copy.start()
    return copy


def stepped(items, moment):
    return (items.astype(F32) - learn_rate * moment.astype(F32)).astype(BF16)


def user_update(mis, items, u, p, scale):
    total = lax.dot_general(mis, items, (((1,), (1,)), ((), ())), preferred_element_type=F32)
    old = u.astype(F32)
    wide = jnp.concatenate([scale] * (u.shape[1] // LANES), axis=1)
    moment = moment_rate * p + (total * wide + decay_rate * old)
    return (old - learn_rate * moment).astype(BF16), moment


def main_kernel(
    n_outer, n_inner,
    x_hbm, w_hbm, uc_hbm, ic_hbm, u_hbm, p_hbm, v_hbm, q_hbm,
    u, p, rcu, mis, v_last, vn_last, qn_last,
    x, w, uc, ic, ut, v0, q0, vt, qt, vp, vn, qn, counts,
    x_sem, w_sem, in_sem, send_sem, recv_sem,
):
    outer = lax.axis_index("outer")
    inner = lax.axis_index("inner")

    def ahead(n):
        return lax.rem(inner + n + n_inner, n_inner)

    right = (outer, ahead(1))
    second = (outer, ahead(2))
    across = (lax.rem(outer + 1, n_outer), inner)
    odd = lax.rem(inner, 2) == 1
    even = jnp.logical_not(odd)

    users, rank = u.shape
    block = v0.shape[0]
    part = block // CHUNKS
    tile = min(TILE, users)
    tiles = users // tile
    chunks = [slice(k * part, (k + 1) * part) for k in range(CHUNKS)]

    def v_at(s):
        return vt.at[s] if s < STEPS - 1 else v_last

    v_load = load(v_hbm, v0, in_sem.at[0])
    u_load = load(u_hbm, u, in_sem.at[1])

    def load_ratings(s):
        cols = slice(s * block, (s + 1) * block)
        return (
            load(x_hbm.at[:, cols], x.at[s], x_sem.at[s]),
            load(w_hbm.at[:, cols], w.at[s], w_sem.at[s]),
        )

    loads = [load_ratings(0)]
    q_load = load(q_hbm, q0, in_sem.at[2])
    ic_load = load(ic_hbm, ic, in_sem.at[3])
    uc_load = load(uc_hbm, uc, in_sem.at[4])
    p_load = load(p_hbm, p, in_sem.at[5])

    barrier = pltpu.get_barrier_semaphore()
    for where in (
        (outer, ahead(-1)), (outer, ahead(-2)), (lax.rem(outer + n_outer - 1, n_outer), inner)
    ):
        pl.semaphore_signal(barrier, inc=1, device_id=where, device_id_type=MESH)

    def remote(kind, s, k, source, target):
        dst = v_at(s) if kind == 0 else (qt, vp)[kind - 1].at[s]
        return pltpu.make_async_remote_copy(
            src_ref=source[0].at[source[1], :, chunks[k]],
            dst_ref=dst.at[:, chunks[k]],
            send_sem=send_sem.at[s, k, kind],
            recv_sem=recv_sem.at[s, k, kind],
            device_id=target,
            device_id_type=MESH,
        )

    always, if_odd, if_even = [], [], []

    def send(bin, *args):
        remote(*args).start()
        bin.append(args)

    v_load.wait()
    vt[0] = v0[...].T
    pl.semaphore_wait(barrier, 3)

    @pl.when(odd)
    def _():
        for k in range(CHUNKS):
            send(if_odd, 2, 1, k, (vt, 0), right)

    u_load.wait()
    for t in range(tiles):
        rows = slice(t * tile, (t + 1) * tile)
        ut[:, rows] = u[rows, :].T
    q_load.wait()
    qt[0] = q0[...].T

    ic_load.wait()
    per = block // LANES
    for s in range(STEPS):
        late = 1 if s >= HALF else 0
        o_from = lax.rem(outer - late + n_outer, n_outer)
        i_from = lax.rem(inner - (s - late) + n_inner * STEPS, n_inner)
        first = (o_from * n_inner + i_from) * per
        for j in range(per):
            row = ic[pl.ds(first + j, 1), :].astype(F32)
            counts[s : s + 1, j * LANES : (j + 1) * LANES] = 1.0 / row
    uc_load.wait()
    flipped = (1.0 / uc[...].astype(F32)).T
    for j in range(users // LANES):
        rcu[j * LANES : (j + 1) * LANES, :] = jnp.broadcast_to(flipped[:, j : j + 1], (LANES, LANES))

    for s in range(STEPS):
        last = s == STEPS - 1
        turn = s == HALF - 1
        loads[s][0].wait()
        loads[s][1].wait()
        if s == 0:
            for n in range(1, STEPS):
                loads.append(load_ratings(n))
        here = v_at(s)
        for k in range(CHUNKS):
            cols = chunks[k]

            def derive():
                remote(2, s, k, (vp, s), right).wait_recv()
                remote(1, s, k, (vp, s), right).wait_recv()
                here[:, cols] = stepped(vp[s, :, cols], qt[s, :, cols])

            if s == HALF:
                derive()
            elif s > 0:
                pl.when(even)(derive)

                @pl.when(odd)
                def _():
                    remote(0, s, k, (vp, s), right).wait_recv()

            if s == HALF:

                @pl.when(odd)
                def _():
                    send(if_odd, 2, s + 1, k, (vt, s), right)

            if turn:
                send(always, 2, s + 1, k, (vt, s), across)
            items = here[:, cols]
            for t in range(tiles):
                rows = slice(t * tile, (t + 1) * tile)
                pred = jnp.dot(u[rows, :], items, preferred_element_type=F32)
                rated = x[s, rows, cols].astype(F32)
                weight = w[s, rows, cols].astype(F32)
                mis[rows, cols] = (weight * (pred - rated)).astype(BF16)
            product = jnp.dot(ut[...], mis[:, cols], preferred_element_type=F32)
            if s > 0 and s != HALF:

                @pl.when(odd)
                def _():
                    remote(1, s, k, (vp, s), right).wait_recv()

            old = items.astype(F32)
            grad = product * counts[s : s + 1, cols] + decay_rate * old
            moment = (moment_rate * qt[s, :, cols].astype(F32) + grad).astype(BF16)
            if last:
                qn_last[:, cols] = moment
                vn_last[:, cols] = stepped(items, moment)
                continue
            qn[s, :, cols] = moment
            if turn:
                send(always, 1, s + 1, k, (qn, s), across)
                continue
            vn[s, :, cols] = stepped(items, moment)

            @pl.when(even)
            def _():
                send(if_even, 0, s + 1, k, (vn, s), right)

            send(always, 1, s + 1, k, (qn, s), right)
            if s % HALF < HALF - 2:

                @pl.when(even)
                def _():
                    send(if_even, 2, s + 2, k, (vn, s), second)

        if last:
            break
        if s == 0:
            p_load.wait()
        for t in range(tiles):
            rows = slice(t * tile, (t + 1) * tile)
            new, p[rows, :] = user_update(mis[rows, :], here[...], u[rows, :], p[rows, :], rcu[rows, :])
            u[rows, :] = new
            ut[:, rows] = new.T

    for args in always:
        remote(*args).wait_send()

    @pl.when(odd)
    def _():
        for args in if_odd:
            remote(*args).wait_send()

    @pl.when(even)
    def _():
        for args in if_even:
            remote(*args).wait_send()


def last_kernel(
    u, p, rcu, mis, v_last, vn_last, qn_last, u_out, p_out, v_out, q_out, u_new, p_new, v_new, q_new, sem
):
    users = u.shape[0]
    tile = min(TILE, users)
    v_new[...] = vn_last[...].T
    outs = [load(v_new, v_out, sem.at[0, 0])]
    q_new[...] = qn_last[...].T
    outs.append(load(q_new, q_out, sem.at[1, 0]))
    for t in range(users // tile):
        rows = slice(t * tile, (t + 1) * tile)
        u_new[rows, :], p_new[rows, :] = user_update(
            mis[rows, :], v_last[...], u[rows, :], p[rows, :], rcu[rows, :]
        )
        outs.append(load(p_new.at[rows], p_out.at[rows], sem.at[2, t]))
        outs.append(load(u_new.at[rows], u_out.at[rows], sem.at[3, t]))
    for copy in outs:
        copy.wait()


def body(ratings, rating_weights, user_counts, item_counts, users, user_moment, items, item_moment):
    n_outer = lax.axis_size("outer")
    n_inner = lax.axis_size("inner")
    n_users, rank = users.shape
    block = items.shape[0]
    n_items = item_counts.shape[0]
    tiles = n_users // min(TILE, n_users)
    i32 = jnp.int32
    args = (
        ratings,
        rating_weights,
        user_counts.reshape(n_users // LANES, LANES),
        item_counts.reshape(n_items // LANES, LANES),
        users,
        user_moment,
        items,
        item_moment,
    )
    vmem = pl.BlockSpec(memory_space=pltpu.VMEM)
    hbm = pl.BlockSpec(memory_space=pltpu.HBM)
    state = pl.pallas_call(
        functools.partial(main_kernel, n_outer, n_inner),
        out_shape=(
            pltpu.VMEM((n_users, rank), BF16),
            pltpu.VMEM((n_users, rank), F32),
            pltpu.VMEM((n_users, LANES), F32),
            pltpu.VMEM((n_users, block), BF16),
            pltpu.VMEM((rank, block), BF16),
            pltpu.VMEM((rank, block), BF16),
            pltpu.VMEM((rank, block), BF16),
        ),
        in_specs=[hbm] * 8,
        out_specs=(vmem,) * 7,
        scratch_shapes=[
            pltpu.VMEM((STEPS, n_users, block), BF16),
            pltpu.VMEM((STEPS, n_users, block), BF16),
            pltpu.VMEM((n_users // LANES, LANES), i32),
            pltpu.VMEM((n_items // LANES, LANES), i32),
            pltpu.VMEM((rank, n_users), BF16),
            pltpu.VMEM((block, rank), BF16),
            pltpu.VMEM((block, rank), BF16),
            pltpu.VMEM((STEPS - 1, rank, block), BF16),
            pltpu.VMEM((STEPS, rank, block), BF16),
            pltpu.VMEM((STEPS, rank, block), BF16),
            pltpu.VMEM((STEPS, rank, block), BF16),
            pltpu.VMEM((STEPS, rank, block), BF16),
            pltpu.VMEM((STEPS, block), F32),
            pltpu.SemaphoreType.DMA((STEPS,)),
            pltpu.SemaphoreType.DMA((STEPS,)),
            pltpu.SemaphoreType.DMA((6,)),
            pltpu.SemaphoreType.DMA((STEPS, CHUNKS, 3)),
            pltpu.SemaphoreType.DMA((STEPS, CHUNKS, 3)),
        ],
        compiler_params=pltpu.CompilerParams(
            collective_id=0, has_side_effects=True, vmem_limit_bytes=32 * 1024 * 1024
        ),
    )(*(pltpu.with_memory_space_constraint(a, pltpu.HBM) for a in args))
    return pl.pallas_call(
        last_kernel,
        out_shape=(
            jax.ShapeDtypeStruct(users.shape, BF16),
            jax.ShapeDtypeStruct(user_moment.shape, F32),
            jax.ShapeDtypeStruct(items.shape, BF16),
            jax.ShapeDtypeStruct(item_moment.shape, BF16),
        ),
        in_specs=[vmem] * 7,
        out_specs=(hbm,) * 4,
        scratch_shapes=[
            pltpu.VMEM((n_users, rank), BF16),
            pltpu.VMEM((n_users, rank), F32),
            pltpu.VMEM((block, rank), BF16),
            pltpu.VMEM((block, rank), BF16),
            pltpu.SemaphoreType.DMA((4, tiles)),
        ],
        compiler_params=pltpu.CompilerParams(vmem_limit_bytes=16 * 1024 * 1024),
    )(*state)


def solution(mesh):
    spread = P(("outer", "inner"), None)
    in_specs = (spread, spread, P(("outer", "inner")), P(), spread, spread, spread, spread)
    return jax.shard_map(
        body, mesh=mesh, in_specs=in_specs, out_specs=(spread,) * 4, check_vma=False
    )
```

time: 43.1 us -> 34.9 us (0.81)
  local copies, waits for them, and re-layouts: 8.58 us -> 0 us
  Pallas kernels: 33.5 us -> 34.1 us
    unnamed x16 -> x0, local copies, waits for them, and re-layouts: 8.58 us -> none
    pallas_call x1 -> x2, Pallas kernels: 33.5 us -> 34.1 us  [the longest x1 32.4 us: body(): pl.pallas_call(functools.partial(main_kernel, n_outer, n_inner), out_shap...]
where the time goes in v1:
time: 34.9 us; the launch traced here: 34.7 us
  Pallas kernels  34.1 us (98%)
  between operations  0.64 us (2%)
    pallas_call x1, Pallas kernels, body(): pl.pallas_call(functools.partial(main_kernel, n_outer, n_inner), out_shap...  32.4 us
    pallas_call x1, Pallas kernels, body(): pl.pallas_call(last_kernel, out_shape=(jax.ShapeDtypeStruct(users.shape,...  1.68 us

profile of v1, /device:TPU:0, one launch (start us, length us, event | category | flops | bytes accessed | tf_op | source)
XLA Modules:
  0.0 34.7 jit_solution(2076650127514616516)
XLA Ops:
  0.6 32.4 %shard_map.111 = (bf16[1024,256]{1,0:T(8,128)(2,1)S(1)}, f32[1024,256]{1,0:T(8,128)S(1)}, f32[1024,128]{1,0:T(8,128)S(1)}, bf16[1024,256]{1,0:T(8,128)(2,1)S(1)}...) custom-call(bf16[1024,2048]{1,0:T(8,128)(2,1)} %x_hbm.1, ...), custom_call_target="tpu_custom_call" | custom-call | tf_op jit(solution)/shard_map/pallas_call | solution.py:276
  33.1 1.7 %shard_map.112 = (bf16[1024,256]{1,0:T(8,128)(2,1)}, f32[1024,256]{1,0:T(8,128)}, bf16[256,256]{1,0:T(8,128)(2,1)}, bf16[256,256]{1,0:T(8,128)(2,1)}) custom-call(bf16[1024,256]{1,0:T(8,128)(2,1)S(1)} %get-tuple-element.11.u, f32[1024,256]{1,0:T(8,128)S(1)} %get-tuple-element.12.p, f32[1024,128]{1,0:T(8,128)S(1)} %get-tuple-element.13.rcu, ...), custom_call_target="tpu_custom_call" | custom-call | tf_op jit(solution)/shard_map/pallas_call | solution.py:313

commit v2 on v1

--- a/solution.py
+++ b/solution.py
@@ -42,8 +42,8 @@
     n_outer, n_inner,
     x_hbm, w_hbm, uc_hbm, ic_hbm, u_hbm, p_hbm, v_hbm, q_hbm,
     u, p, rcu, mis, v_last, vn_last, qn_last,
-    x, w, uc, ic, ut, v0, q0, vt, qt, vp, vn, qn, counts,
-    x_sem, w_sem, in_sem, send_sem, recv_sem,
+    x, w, uc, ic, ut, v0, q0, v_raw, vt, qt, vp, vn, qn, counts,
+    rate_sem, in_sem, send_sem, recv_sem,
 ):
     outer = lax.axis_index("outer")
     inner = lax.axis_index("inner")
@@ -54,6 +54,8 @@
     right = (outer, ahead(1))
     second = (outer, ahead(2))
     across = (lax.rem(outer + 1, n_outer), inner)
+    beyond = (lax.rem(outer + 1, n_outer), ahead(1))
+    behind = lax.rem(outer + n_outer - 1, n_outer)
     odd = lax.rem(inner, 2) == 1
     even = jnp.logical_not(odd)
 
@@ -67,64 +69,66 @@
     def v_at(s):
         return vt.at[s] if s < STEPS - 1 else v_last
 
+    barrier = pltpu.get_barrier_semaphore()
+    sources = ((outer, ahead(-1)), (outer, ahead(-2)), (behind, inner), (behind, ahead(-1)))
+    for where in sources:
+        pl.semaphore_signal(barrier, inc=1, device_id=where, device_id_type=MESH)
+
     v_load = load(v_hbm, v0, in_sem.at[0])
     u_load = load(u_hbm, u, in_sem.at[1])
 
     def load_ratings(s):
         cols = slice(s * block, (s + 1) * block)
         return (
-            load(x_hbm.at[:, cols], x.at[s], x_sem.at[s]),
-            load(w_hbm.at[:, cols], w.at[s], w_sem.at[s]),
+            load(x_hbm.at[:, cols], x.at[s], rate_sem.at[s % 3]),
+            load(w_hbm.at[:, cols], w.at[s], rate_sem.at[s % 3]),
         )
 
     loads = [load_ratings(0)]
     q_load = load(q_hbm, q0, in_sem.at[2])
-    ic_load = load(ic_hbm, ic, in_sem.at[3])
-    uc_load = load(uc_hbm, uc, in_sem.at[4])
-    p_load = load(p_hbm, p, in_sem.at[5])
-
-    barrier = pltpu.get_barrier_semaphore()
-    for where in (
-        (outer, ahead(-1)), (outer, ahead(-2)), (lax.rem(outer + n_outer - 1, n_outer), inner)
-    ):
-        pl.semaphore_signal(barrier, inc=1, device_id=where, device_id_type=MESH)
+    ic_load = load(ic_hbm, ic, in_sem.at[2])
+    uc_load = load(uc_hbm, uc, in_sem.at[3])
+    p_load = load(p_hbm, p, in_sem.at[3])
 
     def remote(kind, s, k, source, target):
         dst = v_at(s) if kind == 0 else (qt, vp)[kind - 1].at[s]
         return pltpu.make_async_remote_copy(
             src_ref=source[0].at[source[1], :, chunks[k]],
             dst_ref=dst.at[:, chunks[k]],
-            send_sem=send_sem.at[s, k, kind],
-            recv_sem=recv_sem.at[s, k, kind],
+            send_sem=send_sem.at[0],
+            recv_sem=recv_sem.at[s - 1, k],
             device_id=target,
             device_id_type=MESH,
         )
 
+    def first_items(k):
+        return pltpu.make_async_remote_copy(
+            src_ref=v_hbm.at[chunks[k]],
+            dst_ref=v_raw.at[chunks[k]],
+            send_sem=send_sem.at[0],
+            recv_sem=recv_sem.at[0, k],
+            device_id=right,
+            device_id_type=MESH,
+        )
+
+    def arrive(s, k):
+        both = vp.at[s, :, : part * 2]
+        pltpu.make_async_copy(both, both, recv_sem.at[s - 1, k]).wait()
+
+    def drain(count):
+        for n in range(count):
+            sent = vp.at[0, :, :part]
+            pltpu.make_async_copy(sent, sent, send_sem.at[0]).wait()
+
     always, if_odd, if_even = [], [], []
 
     def send(bin, *args):
         remote(*args).start()
         bin.append(args)
 
-    v_load.wait()
-    vt[0] = v0[...].T
-    pl.semaphore_wait(barrier, 3)
-
-    @pl.when(odd)
-    def _():
-        for k in range(CHUNKS):
-            send(if_odd, 2, 1, k, (vt, 0), right)
-
-    u_load.wait()
-    for t in range(tiles):
-        rows = slice(t * tile, (t + 1) * tile)
-        ut[:, rows] = u[rows, :].T
-    q_load.wait()
-    qt[0] = q0[...].T
-
-    ic_load.wait()
     per = block // LANES
-    for s in range(STEPS):
+
+    def item_scale(s):
         late = 1 if s >= HALF else 0
         o_from = lax.rem(outer - late + n_outer, n_outer)
         i_from = lax.rem(inner - (s - late) + n_inner * STEPS, n_inner)
@@ -132,37 +136,41 @@
         for j in range(per):
             row = ic[pl.ds(first + j, 1), :].astype(F32)
             counts[s : s + 1, j * LANES : (j + 1) * LANES] = 1.0 / row
-    uc_load.wait()
-    flipped = (1.0 / uc[...].astype(F32)).T
-    for j in range(users // LANES):
-        rcu[j * LANES : (j + 1) * LANES, :] = jnp.broadcast_to(flipped[:, j : j + 1], (LANES, LANES))
+
+    pl.semaphore_wait(barrier, len(sources))
+
+    @pl.when(odd)
+    def _():
+        for k in range(CHUNKS):
+            first_items(k).start()
+
+    v_load.wait()
+    vt[0] = v0[...].T
+    u_load.wait()
+    for t in range(tiles):
+        rows = slice(t * tile, (t + 1) * tile)
+        ut[:, rows] = u[rows, :].T
 
     for s in range(STEPS):
         last = s == STEPS - 1
         turn = s == HALF - 1
         loads[s][0].wait()
         loads[s][1].wait()
-        if s == 0:
-            for n in range(1, STEPS):
-                loads.append(load_ratings(n))
         here = v_at(s)
         for k in range(CHUNKS):
             cols = chunks[k]
 
             def derive():
-                remote(2, s, k, (vp, s), right).wait_recv()
-                remote(1, s, k, (vp, s), right).wait_recv()
-                here[:, cols] = stepped(vp[s, :, cols], qt[s, :, cols])
-
+                before = v_raw[cols, :].T if s == 1 else vp[s, :, cols]
+                here[:, cols] = stepped(before, qt[s, :, cols])
+
+            if s > 0:
+                arrive(s, k)
             if s == HALF:
                 derive()
             elif s > 0:
                 pl.when(even)(derive)
 
-                @pl.when(odd)
-                def _():
-                    remote(0, s, k, (vp, s), right).wait_recv()
-
             if s == HALF:
 
                 @pl.when(odd)
@@ -170,21 +178,28 @@
                     send(if_odd, 2, s + 1, k, (vt, s), right)
 
             if turn:
-                send(always, 2, s + 1, k, (vt, s), across)
+
+                @pl.when(even)
+                def _():
+                    send(if_even, 2, s + 1, k, (vt, s), across)
+
             items = here[:, cols]
-            for t in range(tiles):
+            wide = slice(0, block) if s == 0 else cols
+            for t in range(tiles if s > 0 or k == 0 else 0):
                 rows = slice(t * tile, (t + 1) * tile)
-                pred = jnp.dot(u[rows, :], items, preferred_element_type=F32)
-                rated = x[s, rows, cols].astype(F32)
-                weight = w[s, rows, cols].astype(F32)
-                mis[rows, cols] = (weight * (pred - rated)).astype(BF16)
+                pred = jnp.dot(u[rows, :], here[:, wide], preferred_element_type=F32)
+                rated = x[s, rows, wide].astype(F32)
+                weight = w[s, rows, wide].astype(F32)
+                mis[rows, wide] = (weight * (pred - rated)).astype(BF16)
+            if s == 0 and k == 0:
+                q_load.wait()
+                ic_load.wait()
+                qt[0] = q0[...].T
+                item_scale(0)
+            if k == 0:
+                ahead_of = range(1, 3) if s == 0 else range(s + 2, min(s + 3, STEPS))
+                loads += [load_ratings(n) for n in ahead_of]
             product = jnp.dot(ut[...], mis[:, cols], preferred_element_type=F32)
-            if s > 0 and s != HALF:
-
-                @pl.when(odd)
-                def _():
-                    remote(1, s, k, (vp, s), right).wait_recv()
-
             old = items.astype(F32)
             grad = product * counts[s : s + 1, cols] + decay_rate * old
             moment = (moment_rate * qt[s, :, cols].astype(F32) + grad).astype(BF16)
@@ -203,34 +218,53 @@
                 send(if_even, 0, s + 1, k, (vn, s), right)
 
             send(always, 1, s + 1, k, (qn, s), right)
-            if s % HALF < HALF - 2:
+            if s == HALF - 2:
+
+                @pl.when(even)
+                def _():
+                    send(if_even, 2, s + 2, k, (vn, s), beyond)
+
+            elif 0 < s and s % HALF < HALF - 2:
 
                 @pl.when(even)
                 def _():
                     send(if_even, 2, s + 2, k, (vn, s), second)
 
+
         if last:
             break
+
         if s == 0:
+            for n in range(1, STEPS):
+                item_scale(n)
+            uc_load.wait()
             p_load.wait()
+            flipped = (1.0 / uc[...].astype(F32)).T
+            for j in range(users // LANES):
+                spread = jnp.broadcast_to(flipped[:, j : j + 1], (LANES, LANES))
+                rcu[j * LANES : (j + 1) * LANES, :] = spread
         for t in range(tiles):
             rows = slice(t * tile, (t + 1) * tile)
             new, p[rows, :] = user_update(mis[rows, :], here[...], u[rows, :], p[rows, :], rcu[rows, :])
             u[rows, :] = new
             ut[:, rows] = new.T
 
-    for args in always:
-        remote(*args).wait_send()
+        if s == 0:
+
+            @pl.when(even)
+            def _():
+                for k in range(CHUNKS):
+                    send(if_even, 2, s + 2, k, (vn, s), second)
+
+    drain(len(always))
 
     @pl.when(odd)
     def _():
-        for args in if_odd:
-            remote(*args).wait_send()
+        drain(CHUNKS + len(if_odd))
 
     @pl.when(even)
     def _():
-        for args in if_even:
-            remote(*args).wait_send()
+        drain(len(if_even))
 
 
 def last_kernel(
@@ -239,16 +273,16 @@
     users = u.shape[0]
     tile = min(TILE, users)
     v_new[...] = vn_last[...].T
-    outs = [load(v_new, v_out, sem.at[0, 0])]
+    outs = [load(v_new, v_out, sem.at[0])]
     q_new[...] = qn_last[...].T
-    outs.append(load(q_new, q_out, sem.at[1, 0]))
+    outs.append(load(q_new, q_out, sem.at[0]))
     for t in range(users // tile):
         rows = slice(t * tile, (t + 1) * tile)
         u_new[rows, :], p_new[rows, :] = user_update(
             mis[rows, :], v_last[...], u[rows, :], p[rows, :], rcu[rows, :]
         )
-        outs.append(load(p_new.at[rows], p_out.at[rows], sem.at[2, t]))
-        outs.append(load(u_new.at[rows], u_out.at[rows], sem.at[3, t]))
+        outs.append(load(p_new.at[rows], p_out.at[rows], sem.at[0]))
+        outs.append(load(u_new.at[rows], u_out.at[rows], sem.at[0]))
     for copy in outs:
         copy.wait()
 
@@ -259,7 +293,6 @@
     n_users, rank = users.shape
     block = items.shape[0]
     n_items = item_counts.shape[0]
-    tiles = n_users // min(TILE, n_users)
     i32 = jnp.int32
     args = (
         ratings,
@@ -294,17 +327,17 @@
             pltpu.VMEM((rank, n_users), BF16),
             pltpu.VMEM((block, rank), BF16),
             pltpu.VMEM((block, rank), BF16),
+            pltpu.VMEM((block, rank), BF16),
             pltpu.VMEM((STEPS - 1, rank, block), BF16),
             pltpu.VMEM((STEPS, rank, block), BF16),
             pltpu.VMEM((STEPS, rank, block), BF16),
             pltpu.VMEM((STEPS, rank, block), BF16),
             pltpu.VMEM((STEPS, rank, block), BF16),
             pltpu.VMEM((STEPS, block), F32),
-            pltpu.SemaphoreType.DMA((STEPS,)),
-            pltpu.SemaphoreType.DMA((STEPS,)),
-            pltpu.SemaphoreType.DMA((6,)),
-            pltpu.SemaphoreType.DMA((STEPS, CHUNKS, 3)),
-            pltpu.SemaphoreType.DMA((STEPS, CHUNKS, 3)),
+            pltpu.SemaphoreType.DMA((3,)),
+            pltpu.SemaphoreType.DMA((4,)),
+            pltpu.SemaphoreType.DMA((1,)),
+            pltpu.SemaphoreType.DMA((STEPS - 1, CHUNKS)),
         ],
         compiler_params=pltpu.CompilerParams(
             collective_id=0, has_side_effects=True, vmem_limit_bytes=32 * 1024 * 1024
@@ -325,7 +358,7 @@
             pltpu.VMEM((n_users, rank), F32),
             pltpu.VMEM((block, rank), BF16),
             pltpu.VMEM((block, rank), BF16),
-            pltpu.SemaphoreType.DMA((4, tiles)),
+            pltpu.SemaphoreType.DMA((1,)),
         ],
         compiler_params=pltpu.CompilerParams(vmem_limit_bytes=16 * 1024 * 1024),
     )(*state)

time: 34.9 us -> 33.5 us (0.960)
  Pallas kernels: 34.1 us -> 32.8 us
    pallas_call x1, Pallas kernels: 32.4 us -> 31.2 us  [body(): pl.pallas_call(functools.partial(main_kernel, n_outer, n_inner), out_shap...]
where the time goes in v2:
time: 33.5 us; the launch traced here: 33.4 us
  Pallas kernels  32.8 us (98%)
  between operations  0.64 us (2%)
    pallas_call x1, Pallas kernels, body(): pl.pallas_call(functools.partial(main_kernel, n_outer, n_inner), out_shap...  31.2 us
    pallas_call x1, Pallas kernels, body(): pl.pallas_call(last_kernel, out_shape=(jax.ShapeDtypeStruct(users.shape,...  1.53 us

profile of v2, /device:TPU:0, one launch (start us, length us, event | category | flops | bytes accessed | tf_op | source)
XLA Modules:
  0.0 33.4 jit_solution(9878171929729867131)
XLA Ops:
  0.6 31.2 %shard_map.111 = (bf16[1024,256]{1,0:T(8,128)(2,1)S(1)}, f32[1024,256]{1,0:T(8,128)S(1)}, f32[1024,128]{1,0:T(8,128)S(1)}, bf16[1024,256]{1,0:T(8,128)(2,1)S(1)}...) custom-call(bf16[1024,2048]{1,0:T(8,128)(2,1)} %x_hbm.1, ...), custom_call_target="tpu_custom_call" | custom-call | tf_op jit(solution)/shard_map/pallas_call | solution.py:309
  31.9 1.5 %shard_map.112 = (bf16[1024,256]{1,0:T(8,128)(2,1)}, f32[1024,256]{1,0:T(8,128)}, bf16[256,256]{1,0:T(8,128)(2,1)}, bf16[256,256]{1,0:T(8,128)(2,1)}) custom-call(bf16[1024,256]{1,0:T(8,128)(2,1)S(1)} %get-tuple-element.11.u, f32[1024,256]{1,0:T(8,128)S(1)} %get-tuple-element.12.p, f32[1024,128]{1,0:T(8,128)S(1)} %get-tuple-element.13.rcu, ...), custom_call_target="tpu_custom_call" | custom-call | tf_op jit(solution)/shard_map/pallas_call | solution.py:346

commit v3 on v2

--- a/solution.py
+++ b/solution.py
@@ -87,8 +87,6 @@
     loads = [load_ratings(0)]
     q_load = load(q_hbm, q0, in_sem.at[2])
     ic_load = load(ic_hbm, ic, in_sem.at[2])
-    uc_load = load(uc_hbm, uc, in_sem.at[3])
-    p_load = load(p_hbm, p, in_sem.at[3])
 
     def remote(kind, s, k, source, target):
         dst = v_at(s) if kind == 0 else (qt, vp)[kind - 1].at[s]
@@ -156,6 +154,9 @@
         turn = s == HALF - 1
         loads[s][0].wait()
         loads[s][1].wait()
+        if s == 0:
+            uc_load = load(uc_hbm, uc, in_sem.at[3])
+            p_load = load(p_hbm, p, in_sem.at[3])
         here = v_at(s)
         for k in range(CHUNKS):
             cols = chunks[k]
@@ -197,7 +198,7 @@
                 qt[0] = q0[...].T
                 item_scale(0)
             if k == 0:
-                ahead_of = range(1, 3) if s == 0 else range(s + 2, min(s + 3, STEPS))
+                ahead_of = range(1, 2) if s == 0 else range(s + 2, min(s + 3, STEPS))
                 loads += [load_ratings(n) for n in ahead_of]
             product = jnp.dot(ut[...], mis[:, cols], preferred_element_type=F32)
             old = items.astype(F32)
@@ -250,6 +251,7 @@
             ut[:, rows] = new.T
 
         if s == 0:
+            loads.append(load_ratings(2))
 
             @pl.when(even)
             def _():
@@ -271,7 +273,7 @@
     u, p, rcu, mis, v_last, vn_last, qn_last, u_out, p_out, v_out, q_out, u_new, p_new, v_new, q_new, sem
 ):
     users = u.shape[0]
-    tile = min(TILE, users)
+    tile = min(TILE // 2, users)
     v_new[...] = vn_last[...].T
     outs = [load(v_new, v_out, sem.at[0])]
     q_new[...] = qn_last[...].T

time: 33.5 us -> 33.1 us (0.988)
  Pallas kernels: 32.8 us -> 32.3 us
where the time goes in v3:
time: 33.1 us; the launch traced here: 33 us
  Pallas kernels  32.3 us (98%)
  between operations  0.64 us (2%)
    pallas_call x1, Pallas kernels, body(): pl.pallas_call(functools.partial(main_kernel, n_outer, n_inner), out_shap...  30.9 us
    pallas_call x1, Pallas kernels, body(): pl.pallas_call(last_kernel, out_shape=(jax.ShapeDtypeStruct(users.shape,...  1.4 us

profile of v3, /device:TPU:0, one launch (start us, length us, event | category | flops | bytes accessed | tf_op | source)
XLA Modules:
  0.0 33.0 jit_solution(14524647039783641494)
XLA Ops:
  0.6 30.9 %shard_map.111 = (bf16[1024,256]{1,0:T(8,128)(2,1)S(1)}, f32[1024,256]{1,0:T(8,128)S(1)}, f32[1024,128]{1,0:T(8,128)S(1)}, bf16[1024,256]{1,0:T(8,128)(2,1)S(1)}...) custom-call(bf16[1024,2048]{1,0:T(8,128)(2,1)} %x_hbm.1, ...), custom_call_target="tpu_custom_call" | custom-call | tf_op jit(solution)/shard_map/pallas_call | solution.py:311
  31.6 1.4 %shard_map.112 = (bf16[1024,256]{1,0:T(8,128)(2,1)}, f32[1024,256]{1,0:T(8,128)}, bf16[256,256]{1,0:T(8,128)(2,1)}, bf16[256,256]{1,0:T(8,128)(2,1)}) custom-call(bf16[1024,256]{1,0:T(8,128)(2,1)S(1)} %get-tuple-element.11.u, f32[1024,256]{1,0:T(8,128)S(1)} %get-tuple-element.12.p, f32[1024,128]{1,0:T(8,128)S(1)} %get-tuple-element.13.rcu, ...), custom_call_target="tpu_custom_call" | custom-call | tf_op jit(solution)/shard_map/pallas_call | solution.py:348

commit v4 on v3

--- a/solution.py
+++ b/solution.py
@@ -38,11 +38,18 @@
     return (old - learn_rate * moment).astype(BF16), moment
 
 
+def item_update(ut, mis, items, moment, scale):
+    product = jnp.dot(ut, mis, preferred_element_type=F32)
+    grad = product * scale + decay_rate * items.astype(F32)
+    moment = (moment_rate * moment.astype(F32) + grad).astype(BF16)
+    return stepped(items, moment), moment
+
+
 def main_kernel(
     n_outer, n_inner,
     x_hbm, w_hbm, uc_hbm, ic_hbm, u_hbm, p_hbm, v_hbm, q_hbm,
-    u, p, rcu, mis, v_last, vn_last, qn_last,
-    x, w, uc, ic, ut, v0, q0, v_raw, vt, qt, vp, vn, qn, counts,
+    u, p, rcu, mis, v_last, vn_last, qn_last, ut, q_last, counts,
+    x, w, uc, ic, v0, q0, v_raw, vt, qt, vp, vn, qn,
     rate_sem, in_sem, send_sem, recv_sem,
 ):
     outer = lax.axis_index("outer")
@@ -69,6 +76,9 @@
     def v_at(s):
         return vt.at[s] if s < STEPS - 1 else v_last
 
+    def q_at(s):
+        return qt.at[s] if s < STEPS - 1 else q_last
+
     barrier = pltpu.get_barrier_semaphore()
     sources = ((outer, ahead(-1)), (outer, ahead(-2)), (behind, inner), (behind, ahead(-1)))
     for where in sources:
@@ -89,7 +99,7 @@
     ic_load = load(ic_hbm, ic, in_sem.at[2])
 
     def remote(kind, s, k, source, target):
-        dst = v_at(s) if kind == 0 else (qt, vp)[kind - 1].at[s]
+        dst = (v_at(s), q_at(s), vp.at[s])[kind]
         return pltpu.make_async_remote_copy(
             src_ref=source[0].at[source[1], :, chunks[k]],
             dst_ref=dst.at[:, chunks[k]],
@@ -163,7 +173,7 @@
 
             def derive():
                 before = v_raw[cols, :].T if s == 1 else vp[s, :, cols]
-                here[:, cols] = stepped(before, qt[s, :, cols])
+                here[:, cols] = stepped(before, q_at(s)[:, cols])
 
             if s > 0:
                 arrive(s, k)
@@ -200,19 +210,18 @@
             if k == 0:
                 ahead_of = range(1, 2) if s == 0 else range(s + 2, min(s + 3, STEPS))
                 loads += [load_ratings(n) for n in ahead_of]
-            product = jnp.dot(ut[...], mis[:, cols], preferred_element_type=F32)
-            old = items.astype(F32)
-            grad = product * counts[s : s + 1, cols] + decay_rate * old
-            moment = (moment_rate * qt[s, :, cols].astype(F32) + grad).astype(BF16)
+            if last and k == CHUNKS - 1:
+                break
+            new_items, moment = item_update(ut[...], mis[:, cols], items, q_at(s)[:, cols], counts[s : s + 1, cols])
             if last:
                 qn_last[:, cols] = moment
-                vn_last[:, cols] = stepped(items, moment)
+                vn_last[:, cols] = new_items
                 continue
             qn[s, :, cols] = moment
             if turn:
                 send(always, 1, s + 1, k, (qn, s), across)
                 continue
-            vn[s, :, cols] = stepped(items, moment)
+            vn[s, :, cols] = new_items
 
             @pl.when(even)
             def _():
@@ -270,21 +279,42 @@
 
 
 def last_kernel(
-    u, p, rcu, mis, v_last, vn_last, qn_last, u_out, p_out, v_out, q_out, u_new, p_new, v_new, q_new, sem
+    u, p, rcu, mis, v_last, vn_last, qn_last, ut, q_last, counts,
+    u_out, p_out, v_out, q_out, u_new, p_new, v_new, q_new, sem,
 ):
     users = u.shape[0]
+    block = v_last.shape[1]
     tile = min(TILE // 2, users)
-    v_new[...] = vn_last[...].T
-    outs = [load(v_new, v_out, sem.at[0])]
-    q_new[...] = qn_last[...].T
-    outs.append(load(q_new, q_out, sem.at[0]))
-    for t in range(users // tile):
+    tiles = users // tile
+    done = block - block // CHUNKS
+    outs = []
+
+    def user_tile(t):
         rows = slice(t * tile, (t + 1) * tile)
         u_new[rows, :], p_new[rows, :] = user_update(
             mis[rows, :], v_last[...], u[rows, :], p[rows, :], rcu[rows, :]
         )
         outs.append(load(p_new.at[rows], p_out.at[rows], sem.at[0]))
         outs.append(load(u_new.at[rows], u_out.at[rows], sem.at[0]))
+
+    def items_out(rows):
+        outs.append(load(v_new.at[rows], v_out.at[rows], sem.at[0]))
+        outs.append(load(q_new.at[rows], q_out.at[rows], sem.at[0]))
+
+    first, rest = slice(0, done), slice(done, block)
+    v_new[first, :] = vn_last[:, first].T
+    q_new[first, :] = qn_last[:, first].T
+    items_out(first)
+    for t in range(tiles // 2):
+        user_tile(t)
+    new_items, moment = item_update(
+        ut[...], mis[:, rest], v_last[:, rest], q_last[:, rest], counts[STEPS - 1 : STEPS, rest]
+    )
+    v_new[rest, :] = new_items.T
+    q_new[rest, :] = moment.T
+    items_out(rest)
+    for t in range(tiles // 2, tiles):
+        user_tile(t)
     for copy in outs:
         copy.wait()
 
@@ -318,15 +348,17 @@
             pltpu.VMEM((rank, block), BF16),
             pltpu.VMEM((rank, block), BF16),
             pltpu.VMEM((rank, block), BF16),
+            pltpu.VMEM((rank, n_users), BF16),
+            pltpu.VMEM((rank, block), BF16),
+            pltpu.VMEM((STEPS, block), F32),
         ),
         in_specs=[hbm] * 8,
-        out_specs=(vmem,) * 7,
+        out_specs=(vmem,) * 10,
         scratch_shapes=[
             pltpu.VMEM((STEPS, n_users, block), BF16),
             pltpu.VMEM((STEPS, n_users, block), BF16),
             pltpu.VMEM((n_users // LANES, LANES), i32),
             pltpu.VMEM((n_items // LANES, LANES), i32),
-            pltpu.VMEM((rank, n_users), BF16),
             pltpu.VMEM((block, rank), BF16),
             pltpu.VMEM((block, rank), BF16),
             pltpu.VMEM((block, rank), BF16),
@@ -335,7 +367,6 @@
             pltpu.VMEM((STEPS, rank, block), BF16),
             pltpu.VMEM((STEPS, rank, block), BF16),
             pltpu.VMEM((STEPS, rank, block), BF16),
-            pltpu.VMEM((STEPS, block), F32),
             pltpu.SemaphoreType.DMA((3,)),
             pltpu.SemaphoreType.DMA((4,)),
             pltpu.SemaphoreType.DMA((1,)),
@@ -353,7 +384,7 @@
             jax.ShapeDtypeStruct(items.shape, BF16),
             jax.ShapeDtypeStruct(item_moment.shape, BF16),
         ),
-        in_specs=[vmem] * 7,
+        in_specs=[vmem] * 10,
         out_specs=(hbm,) * 4,
         scratch_shapes=[
             pltpu.VMEM((n_users, rank), BF16),

time: 33.1 us -> 33.1 us (level)
  no operation moved by 1% of the time
where the time goes in v4:
time: 33.1 us; the launch traced here: 32.9 us
  Pallas kernels  32.3 us (98%)
  between operations  0.64 us (2%)
    pallas_call x1, Pallas kernels, body(): pl.pallas_call(functools.partial(main_kernel, n_outer, n_inner), out_shap...  30.7 us
    pallas_call x1, Pallas kernels, body(): pl.pallas_call(last_kernel, out_shape=(jax.ShapeDtypeStruct(users.shape,...  1.59 us

profile of v4, /device:TPU:0, one launch (start us, length us, event | category | flops | bytes accessed | tf_op | source)
XLA Modules:
  0.0 32.9 jit_solution(7253778154635671081)
XLA Ops:
  0.6 30.7 %shard_map.111 = (bf16[1024,256]{1,0:T(8,128)(2,1)S(1)}, f32[1024,256]{1,0:T(8,128)S(1)}, f32[1024,128]{1,0:T(8,128)S(1)}, bf16[1024,256]{1,0:T(8,128)(2,1)S(1)}...) custom-call(bf16[1024,2048]{1,0:T(8,128)(2,1)} %x_hbm.1, ...), custom_call_target="tpu_custom_call" | custom-call | tf_op jit(solution)/shard_map/pallas_call | solution.py:341
  31.3 1.6 %shard_map.112 = (bf16[1024,256]{1,0:T(8,128)(2,1)}, f32[1024,256]{1,0:T(8,128)}, bf16[256,256]{1,0:T(8,128)(2,1)}, bf16[256,256]{1,0:T(8,128)(2,1)}) custom-call(bf16[1024,256]{1,0:T(8,128)(2,1)S(1)} %get-tuple-element.14.u, f32[1024,256]{1,0:T(8,128)S(1)} %get-tuple-element.15.p, f32[1024,128]{1,0:T(8,128)S(1)} %get-tuple-element.16.rcu, ...), custom_call_target="tpu_custom_call" | custom-call | tf_op jit(solution)/shard_map/pallas_call | solution.py:379

commit v5 on v4

--- a/solution.py
+++ b/solution.py
@@ -80,7 +80,8 @@
         return qt.at[s] if s < STEPS - 1 else q_last
 
     barrier = pltpu.get_barrier_semaphore()
-    sources = ((outer, ahead(-1)), (outer, ahead(-2)), (behind, inner), (behind, ahead(-1)))
+    early = (jnp.where(odd, behind, outer), jnp.where(odd, ahead(-1), ahead(-2)))
+    sources = ((outer, ahead(-1)), (behind, inner), early)
     for where in sources:
         pl.semaphore_signal(barrier, inc=1, device_id=where, device_id_type=MESH)
 
@@ -145,7 +146,7 @@
             row = ic[pl.ds(first + j, 1), :].astype(F32)
             counts[s : s + 1, j * LANES : (j + 1) * LANES] = 1.0 / row
 
-    pl.semaphore_wait(barrier, len(sources))
+    pl.semaphore_wait(barrier, jnp.where(odd, 2, 4))
 
     @pl.when(odd)
     def _():

time: 33.1 us -> 33.1 us (level)
  no operation moved by 1% of the time
where the time goes in v5:
time: 33.1 us; the launch traced here: 32.9 us
  Pallas kernels  32.3 us (98%)
  between operations  0.64 us (2%)
    pallas_call x1, Pallas kernels, body(): pl.pallas_call(functools.partial(main_kernel, n_outer, n_inner), out_shap...  30.7 us
    pallas_call x1, Pallas kernels, body(): pl.pallas_call(last_kernel, out_shape=(jax.ShapeDtypeStruct(users.shape,...  1.59 us

profile of v5, /device:TPU:0, one launch (start us, length us, event | category | flops | bytes accessed | tf_op | source)
XLA Modules:
  0.0 32.9 jit_solution(12666864239013068724)
XLA Ops:
  0.6 30.7 %shard_map.111 = (bf16[1024,256]{1,0:T(8,128)(2,1)S(1)}, f32[1024,256]{1,0:T(8,128)S(1)}, f32[1024,128]{1,0:T(8,128)S(1)}, bf16[1024,256]{1,0:T(8,128)(2,1)S(1)}...) custom-call(bf16[1024,2048]{1,0:T(8,128)(2,1)} %x_hbm.1, ...), custom_call_target="tpu_custom_call" | custom-call | tf_op jit(solution)/shard_map/pallas_call | solution.py:342
  31.3 1.6 %shard_map.112 = (bf16[1024,256]{1,0:T(8,128)(2,1)}, f32[1024,256]{1,0:T(8,128)}, bf16[256,256]{1,0:T(8,128)(2,1)}, bf16[256,256]{1,0:T(8,128)(2,1)}) custom-call(bf16[1024,256]{1,0:T(8,128)(2,1)S(1)} %get-tuple-element.14.u, f32[1024,256]{1,0:T(8,128)S(1)} %get-tuple-element.15.p, f32[1024,128]{1,0:T(8,128)S(1)} %get-tuple-element.16.rcu, ...), custom_call_target="tpu_custom_call" | custom-call | tf_op jit(solution)/shard_map/pallas_call | solution.py:380
